TPU v7x, 32 devices: a whole 2x2x4 slice. The times are simulated.
32 devices in a mesh: row: 8 (over y, x, core), col: 4 (over z).
Axes of the slice: x: 2, y: 2, z: 4, core: 2. Of those that a mesh axis runs over, the one named last changes fastest.
Arguments:
- weights: int32 [4096, 4096], P('row', 'col'), may hold values from 1 to 64
Outputs:
- distances: int32 [4096, 4096], P('row', 'col')
All inputs are finite; a program needn't handle non-finite values.
Results may differ from a plain program's by a relative error of at most 0.000001.
Values may be sent and summed in bfloat16 or wider, within the bound.
A program may use at most 64 MiB of HBM per device.

v0:
```python
import jax
import jax.numpy as jnp
from jax import lax
from jax.sharding import PartitionSpec as P

PIVOT = 128
STEPS = 4


def broadcast(value, axis, source):
    kept = jnp.where(lax.axis_index(axis) == source, value, 0).astype(value.dtype)
    return lax.psum(kept, axis)


def min_plus(acc, left, right):
    group = 8
    count = left.shape[1] // group

    def update(index, total):
        begin = (index * group).astype(jnp.int32)
        left_part = lax.dynamic_slice_in_dim(left, begin, group, 1)
        right_part = lax.dynamic_slice_in_dim(right, begin, group, 0)
        return jnp.minimum(total, jnp.min(left_part[:, :, None] + right_part[None, :, :], axis=1))

    return lax.fori_loop(0, count, update, acc)


def close_block(block):

    def relax(vertex, current):
        vertex = jnp.asarray(vertex).astype(jnp.int32)
        column = lax.dynamic_slice_in_dim(current, vertex, 1, 1)
        across = lax.dynamic_slice_in_dim(current, vertex, 1, 0)
        return jnp.minimum(current, column + across)

    return lax.fori_loop(0, block.shape[0], relax, block)


def per_device(weights):
    rows_dev, cols_dev = weights.shape
    verts = rows_dev * lax.axis_size("row")
    stride = verts // STEPS
    row_ids = lax.axis_index("row") * rows_dev + jnp.arange(rows_dev, dtype=jnp.int32)
    col_ids = lax.axis_index("col") * cols_dev + jnp.arange(cols_dev, dtype=jnp.int32)
    dist = jnp.where(row_ids[:, None] == col_ids[None, :], jnp.int32(0), weights).astype(jnp.int32)
    for step in range(STEPS):
        first = step * stride
        row_root = first // rows_dev
        row_off = first - row_root * rows_dev
        col_root = first // cols_dev
        col_off = first - col_root * cols_dev
        strip_rows = dist[row_off : row_off + PIVOT, :]
        strip_cols = dist[:, col_off : col_off + PIVOT]
        panel_rows = jax.tree.map(lambda part: broadcast(part, "row", row_root), strip_rows)
        closed = close_block(panel_rows[:, col_off : col_off + PIVOT])
        new_cols = min_plus(strip_cols, strip_cols, closed)
        panel_cols = jax.tree.map(lambda part: broadcast(part, "col", col_root), new_cols)
        dist = min_plus(dist, panel_cols, panel_rows)
    return dist


def solution(mesh):
    placed = (P("row", "col"),)
    return jax.shard_map(
        per_device, mesh=mesh, in_specs=placed, out_specs=P("row", "col"), check_vma=False
    )
```

profile of v0, /device:TPU:0, one launch (start us, length us, event | category | flops | bytes accessed | tf_op | source)
XLA Modules:
  0.0 1356.6 jit_solution(568644067238902018)
XLA Ops:
  9.3 58.6 %all-reduce.9.cloned.1.call-done = s32[128,1024]{1,0:T(8,128)} async-done(((s32[128,1024]{1,0:T(8,128)}), s32[128,1024]{1,0:T(8,128)}) %all-reduce.9.cloned.1.call-update) | async-done | bytes 524304 | tf_op jit(solution)/shard_map/psum | solution.py:12
  68.8 40.3 %while.156 = (s32[]{:T(128)}, s32[128,128]{1,0:T(8,128)S(1)}, s32[]{:T(128)}) while((s32[]{:T(128)}, s32[128,128]{1,0:T(8,128)S(1)}, s32[]{:T(128)}) %tuple.281), condition=%wide.region_2.3_spmd, body=%wide.region_1.2_spmd.sunk | while | flops 32770 | bytes 134197 | solution.py:36
  109.2 50.6 %while.157 = (s32[]{:T(128)}, s32[512,128]{1,0:T(8,128)S(1)}, s32[512,128]{1,0:T(8,128)S(1)}, s32[128,128]{1,0:T(8,128)S(1)}, s32[]{:T(128)}, /*index=5*/s32[]{:T(128)}, s32[]{:T(128)}, s32[]{:T(128)}) while((s32[]{:T(128)}, s32[512,128]{1,0:T(8,128)S(1)}, s32[512,128]{1,0:T(8,128)S(1)}, s32[128,128]{1,0:T(8,128)S(1)}, s32[]{:T(128)}, ...), condition=%wide.region_5.6_spmd, body=%wide.region_3.5_spmd.sunk | while | flops 1048582 | bytes 1110155 | solution.py:25
  160.6 34.8 %all-reduce.11.cloned.1.call-done = s32[512,128]{1,0:T(8,128)} async-done(((s32[512,128]{1,0:T(8,128)}), s32[512,128]{1,0:T(8,128)}) %all-reduce.11.cloned.1.call-update) | async-done | bytes 262160 | tf_op jit(solution)/shard_map/psum | solution.py:12
  195.4 150.9 %while.158 = (s32[]{:T(128)}, s32[512,1024]{1,0:T(8,128)S(1)}, s32[512,128]{1,0:T(8,128)}, s32[128,1024]{1,0:T(8,128)}, s32[]{:T(128)}, /*index=5*/s32[]{:T(128)}, s32[]{:T(128)}, s32[]{:T(128)}) while((s32[]{:T(128)}, s32[512,1024]{1,0:T(8,128)S(1)}, s32[512,128]{1,0:T(8,128)}, s32[128,1024]{1,0:T(8,128)}, s32[]{:T(128)}, ...), condition=%wide.region_9.10_spmd, body=%wide.region_7.9_spmd.sunk | while | flops 8388614 | bytes 8536203 | solution.py:25
  329.3 6.9 add_reduce_fusion.17
  338.7 6.9 add_reduce_fusion.17
  347.3 54.7 %all-reduce.13.cloned.1.call-done = s32[128,1024]{1,0:T(8,128)} async-done(((s32[128,1024]{1,0:T(8,128)}), s32[128,1024]{1,0:T(8,128)}) %all-reduce.13.cloned.1.call-update) | async-done | bytes 524304 | tf_op jit(solution)/shard_map/psum | solution.py:12
  402.9 40.3 %while.159 = (s32[]{:T(128)}, s32[128,128]{1,0:T(8,128)S(1)}, s32[]{:T(128)}) while((s32[]{:T(128)}, s32[128,128]{1,0:T(8,128)S(1)}, s32[]{:T(128)}) %tuple.290), condition=%wide.region_12.13_spmd, body=%wide.region_11.12_spmd.sunk | while | flops 32770 | bytes 134197 | solution.py:36
  443.2 50.6 %while.160 = (s32[]{:T(128)}, s32[512,128]{1,0:T(8,128)S(1)}, s32[512,128]{1,0:T(8,128)S(1)}, s32[128,128]{1,0:T(8,128)S(1)}, s32[]{:T(128)}, /*index=5*/s32[]{:T(128)}, s32[]{:T(128)}, s32[]{:T(128)}) while((s32[]{:T(128)}, s32[512,128]{1,0:T(8,128)S(1)}, s32[512,128]{1,0:T(8,128)S(1)}, s32[128,128]{1,0:T(8,128)S(1)}, s32[]{:T(128)}, ...), condition=%wide.region_15.16_spmd, body=%wide.region_13.15_spmd.sunk | while | flops 1048582 | bytes 1110155 | solution.py:25
  494.6 34.8 %all-reduce.15.cloned.1.call-done = s32[512,128]{1,0:T(8,128)} async-done(((s32[512,128]{1,0:T(8,128)}), s32[512,128]{1,0:T(8,128)}) %all-reduce.15.cloned.1.call-update) | async-done | bytes 262160 | tf_op jit(solution)/shard_map/psum | solution.py:12
  529.5 150.9 %while.161 = (s32[]{:T(128)}, s32[512,1024]{1,0:T(8,128)S(1)}, s32[512,128]{1,0:T(8,128)}, s32[128,1024]{1,0:T(8,128)}, s32[]{:T(128)}, /*index=5*/s32[]{:T(128)}, s32[]{:T(128)}, s32[]{:T(128)}) while((s32[]{:T(128)}, s32[512,1024]{1,0:T(8,128)S(1)}, s32[512,128]{1,0:T(8,128)}, s32[128,1024]{1,0:T(8,128)}, s32[]{:T(128)}, ...), condition=%wide.region_19.20_spmd, body=%wide.region_17.19_spmd.sunk | while | flops 8388614 | bytes 8536203 | solution.py:25
  559.6 6.9 add_reduce_fusion.19
  569.0 6.9 add_reduce_fusion.19
  578.5 6.9 add_reduce_fusion.19
  587.9 6.9 add_reduce_fusion.19
  597.3 6.9 add_reduce_fusion.19
  681.3 54.7 %all-reduce.17.cloned.1.call-done = s32[128,1024]{1,0:T(8,128)} async-done(((s32[128,1024]{1,0:T(8,128)}), s32[128,1024]{1,0:T(8,128)}) %all-reduce.17.cloned.1.call-update) | async-done | bytes 524304 | tf_op jit(solution)/shard_map/psum | solution.py:12
  736.9 40.3 %while.162 = (s32[]{:T(128)}, s32[128,128]{1,0:T(8,128)S(1)}, s32[]{:T(128)}) while((s32[]{:T(128)}, s32[128,128]{1,0:T(8,128)S(1)}, s32[]{:T(128)}) %tuple.299), condition=%wide.region_22.23_spmd, body=%wide.region_21.22_spmd.sunk | while | flops 32770 | bytes 134197 | solution.py:36
  777.2 50.6 %while.163 = (s32[]{:T(128)}, s32[512,128]{1,0:T(8,128)S(1)}, s32[512,128]{1,0:T(8,128)S(1)}, s32[128,128]{1,0:T(8,128)S(1)}, s32[]{:T(128)}, /*index=5*/s32[]{:T(128)}, s32[]{:T(128)}, s32[]{:T(128)}) while((s32[]{:T(128)}, s32[512,128]{1,0:T(8,128)S(1)}, s32[512,128]{1,0:T(8,128)S(1)}, s32[128,128]{1,0:T(8,128)S(1)}, s32[]{:T(128)}, ...), condition=%wide.region_25.26_spmd, body=%wide.region_23.25_spmd.sunk | while | flops 1048582 | bytes 1110155 | solution.py:25
  828.9 34.6 %all-reduce.19.cloned.1.call-done = s32[512,128]{1,0:T(8,128)} async-done(((s32[512,128]{1,0:T(8,128)}), s32[512,128]{1,0:T(8,128)}) %all-reduce.19.cloned.1.call-update) | async-done | bytes 262160 | tf_op jit(solution)/shard_map/psum | solution.py:12
  863.5 150.9 %while.164 = (s32[]{:T(128)}, s32[512,1024]{1,0:T(8,128)S(1)}, s32[512,128]{1,0:T(8,128)}, s32[128,1024]{1,0:T(8,128)}, s32[]{:T(128)}, /*index=5*/s32[]{:T(128)}, s32[]{:T(128)}, s32[]{:T(128)}) while((s32[]{:T(128)}, s32[512,1024]{1,0:T(8,128)S(1)}, s32[512,128]{1,0:T(8,128)}, s32[128,1024]{1,0:T(8,128)}, s32[]{:T(128)}, ...), condition=%wide.region_29.30_spmd, body=%wide.region_27.29_spmd.sunk | while | flops 8388614 | bytes 8536203 | solution.py:25
  969.1 6.9 add_reduce_fusion.21
  978.5 6.9 add_reduce_fusion.21
  988.0 6.9 add_reduce_fusion.21
  997.4 6.9 add_reduce_fusion.21
  1006.8 6.9 add_reduce_fusion.21
  1015.4 54.7 %all-reduce.21.cloned.1.call-done = s32[128,1024]{1,0:T(8,128)} async-done(((s32[128,1024]{1,0:T(8,128)}), s32[128,1024]{1,0:T(8,128)}) %all-reduce.21.cloned.1.call-update) | async-done | bytes 524304 | tf_op jit(solution)/shard_map/psum | solution.py:12
  1071.0 40.3 %while.165 = (s32[]{:T(128)}, s32[128,128]{1,0:T(8,128)S(1)}, s32[]{:T(128)}) while((s32[]{:T(128)}, s32[128,128]{1,0:T(8,128)S(1)}, s32[]{:T(128)}) %tuple.308), condition=%wide.region_32.33_spmd, body=%wide.region_31.32_spmd.sunk | while | flops 32770 | bytes 134197 | solution.py:36
  1111.3 50.6 %while.166 = (s32[]{:T(128)}, s32[512,128]{1,0:T(8,128)S(1)}, s32[512,128]{1,0:T(8,128)S(1)}, s32[128,128]{1,0:T(8,128)S(1)}, s32[]{:T(128)}, /*index=5*/s32[]{:T(128)}, s32[]{:T(128)}, s32[]{:T(128)}) while((s32[]{:T(128)}, s32[512,128]{1,0:T(8,128)S(1)}, s32[512,128]{1,0:T(8,128)S(1)}, s32[128,128]{1,0:T(8,128)S(1)}, s32[]{:T(128)}, ...), condition=%wide.region_35.36_spmd, body=%wide.region_33.35_spmd.sunk | while | flops 1048582 | bytes 1110155 | solution.py:25
  1162.7 34.9 %all-reduce.23.cloned.1.call-done = s32[512,128]{1,0:T(8,128)} async-done(((s32[512,128]{1,0:T(8,128)}), s32[512,128]{1,0:T(8,128)}) %all-reduce.23.cloned.1.call-update) | async-done | bytes 262160 | tf_op jit(solution)/shard_map/psum | solution.py:12
  1197.5 150.9 %while.167 = (s32[]{:T(128)}, s32[512,1024]{1,0:T(8,128)S(1)}, s32[512,128]{1,0:T(8,128)}, s32[128,1024]{1,0:T(8,128)}, s32[]{:T(128)}, /*index=5*/s32[]{:T(128)}, s32[]{:T(128)}, s32[]{:T(128)}) while((s32[]{:T(128)}, s32[512,1024]{1,0:T(8,128)S(1)}, s32[512,128]{1,0:T(8,128)}, s32[128,1024]{1,0:T(8,128)}, s32[]{:T(128)}, ...), condition=%wide.region_39.40_spmd, body=%wide.region_37.39_spmd.sunk | while | flops 8388614 | bytes 8536203 | solution.py:25
  (2077 shorter events, 874.3 us)
Async XLA Ops:
  6.5 61.4 %all-reduce.9.cloned.1.call-start = ((), (), s32[]{:S(2)}) async-start(), calls=%async_computation | async-start | bytes 1048576 | tf_op jit(solution)/shard_map/psum | solution.py:12
  9.2 186.2 %all-reduce.11.cloned.1.call-start = ((), (), s32[]{:S(2)}) async-start(), calls=%async_computation.1 | async-start | bytes 524288 | tf_op jit(solution)/shard_map/psum | solution.py:12
  160.5 241.5 %all-reduce.13.cloned.1.call-start = ((), (), s32[]{:S(2)}) async-start(), calls=%async_computation.2 | async-start | bytes 1048576 | tf_op jit(solution)/shard_map/psum | solution.py:12
  347.2 182.3 %all-reduce.15.cloned.1.call-start = ((), (), s32[]{:S(2)}) async-start(), calls=%async_computation.3 | async-start | bytes 524288 | tf_op jit(solution)/shard_map/psum | solution.py:12
  494.6 241.5 %all-reduce.17.cloned.1.call-start = ((), (), s32[]{:S(2)}) async-start(), calls=%async_computation.4 | async-start | bytes 1048576 | tf_op jit(solution)/shard_map/psum | solution.py:12
  681.2 182.3 %all-reduce.19.cloned.1.call-start = ((), (), s32[]{:S(2)}) async-start(), calls=%async_computation.5 | async-start | bytes 524288 | tf_op jit(solution)/shard_map/psum | solution.py:12
  828.6 241.5 %all-reduce.21.cloned.1.call-start = ((), (), s32[]{:S(2)}) async-start(), calls=%async_computation.6 | async-start | bytes 1048576 | tf_op jit(solution)/shard_map/psum | solution.py:12
  1015.3 182.3 %all-reduce.23.cloned.1.call-start = ((), (), s32[]{:S(2)}) async-start(), calls=%async_computation.7 | async-start | bytes 524288 | tf_op jit(solution)/shard_map/psum | solution.py:12
  1348.4 1.3 copy-start
Sparse Core Ops, SparseCore 0:
  10.4 57.5 all-reduce.8
  160.7 34.7 all-reduce.10
  347.3 54.6 all-reduce.12
  494.7 34.7 all-reduce.14
  681.3 54.6 all-reduce.16
  828.8 34.7 all-reduce.18
  1015.4 54.6 all-reduce.20
  1162.8 34.7 all-reduce.22
where the time goes:
time: 1360 us
  other arithmetic  730 us (54%)
  waiting for transfers between devices  362 us (27%)
  local copies, waits for them, and re-layouts  226 us (17%)
  loops' own time  23.8 us (2%)
  between operations  13.7 us (1%)
    reduce_min x128, other arithmetic, update(): jnp.min(left_part[:, :, None] + right_part[None, :, :], axis=1)  628 us
    psum x8, waiting for transfers between devices, broadcast(): return lax.psum(kept, axis)  362 us
    dynamic_slice x512, local copies, waits for them, and re-layouts, relax(): column = lax.dynamic_slice_in_dim(current, vertex, 1, 1)  89.7 us
    dynamic_slice x128, local copies, waits for them, and re-layouts, update(): left_part = lax.dynamic_slice_in_dim(left, begin, group, 1)  77 us
    dynamic_slice x128, local copies, waits for them, and re-layouts, update(): right_part = lax.dynamic_slice_in_dim(right, begin, group, 0)  49.8 us
    min x512, other arithmetic, relax(): return jnp.minimum(current, column + across)  49 us
    min x128, other arithmetic, update(): jnp.minimum(total, jnp.min(left_part[:, :, None] + right_part[None, :, :]...  45.4 us
  transfers between devices with their start and end apart: 8, of which 8 were waited for; matrix products, arithmetic and copies ran while one was open for 0% of the time, Pallas kernels for 0%

commit v1 on v0

--- a/solution.py
+++ b/solution.py
@@ -7,9 +7,14 @@
 STEPS = 4
 
 
+def work_the_members_all(s0, axis_name):
+    vec_out = lax.all_gather(s0, axis_name).sum(axis=0)
+    return vec_out
+
+
 def broadcast(value, axis, source):
     kept = jnp.where(lax.axis_index(axis) == source, value, 0).astype(value.dtype)
-    return lax.psum(kept, axis)
+    return work_the_members_all(kept, axis)
 
 
 def min_plus(acc, left, right):

time: 1360 us -> 1160 us (0.85)
  local copies, waits for them, and re-layouts: 226 us -> 114 us
  waiting for transfers between devices: 362 us -> 260 us
  other arithmetic: 730 us -> 746 us
    psum x8 -> x0, waiting for transfers between devices: 362 us -> none  [broadcast(): return lax.psum(kept, axis)]
    all_gather x0 -> x8, waiting for transfers between devices: none -> 259 us  [work_the_members_all(): vec_out = lax.all_gather(s0, axis_name).sum(axis=0)]
    dynamic_slice x128, local copies, waits for them, and re-layouts: 77 us -> 16.1 us  [update(): left_part = lax.dynamic_slice_in_dim(left, begin, group, 1)]
    dynamic_slice x128, local copies, waits for them, and re-layouts: 49.8 us -> 1.45 us  [update(): right_part = lax.dynamic_slice_in_dim(right, begin, group, 0)]
    reduce_sum x0 -> x8, other arithmetic: none -> 15.7 us  [work_the_members_all(): vec_out = lax.all_gather(s0, axis_name).sum(axis=0)]
where the time goes in v1:
time: 1160 us
  other arithmetic  746 us (64%)
  waiting for transfers between devices  260 us (22%)
  local copies, waits for them, and re-layouts  114 us (10%)
  loops' own time  24.4 us (2%)
  between operations  13.8 us (1%)
    reduce_min x128, other arithmetic, update(): jnp.min(left_part[:, :, None] + right_part[None, :, :], axis=1)  628 us
    all_gather x8, waiting for transfers between devices, work_the_members_all(): vec_out = lax.all_gather(s0, axis_name).sum(axis=0)  259 us
    dynamic_slice x512, local copies, waits for them, and re-layouts, relax(): column = lax.dynamic_slice_in_dim(current, vertex, 1, 1)  89.7 us
    min x512, other arithmetic, relax(): return jnp.minimum(current, column + across)  49 us
    min x128, other arithmetic, update(): jnp.minimum(total, jnp.min(left_part[:, :, None] + right_part[None, :, :]...  45.4 us
  transfers between devices with their start and end apart: 8, of which 8 were waited for; matrix products, arithmetic and copies ran while one was open for 0% of the time, Pallas kernels for 0%

profile of v1, /device:TPU:0, one launch (start us, length us, event | category | flops | bytes accessed | tf_op | source)
XLA Modules:
  0.0 1158.2 jit_solution(3867862979090990905)
XLA Ops:
  9.3 39.3 %all-gather.17.cloned.1.call-done = s32[1024,1024]{1,0:T(8,128)} async-done(((s32[128,1024]{1,0:T(8,128)}), s32[1024,1024]{1,0:T(8,128)}) %all-gather.17.cloned.1.call-update) | async-done | bytes 4194320 | tf_op jit(solution)/shard_map/all_gather | solution.py:11
  51.3 40.4 %while.156 = (s32[]{:T(128)}, s32[128,128]{1,0:T(8,128)S(1)}, s32[]{:T(128)}) while((s32[]{:T(128)}, s32[128,128]{1,0:T(8,128)S(1)}, s32[]{:T(128)}) %tuple.281), condition=%wide.region_2.3_spmd, body=%wide.region_1.2_spmd.sunk | while | flops 32770 | bytes 134197 | solution.py:41
  91.7 50.6 %while.157 = (s32[]{:T(128)}, s32[512,128]{1,0:T(8,128)S(1)}, s32[512,128]{1,0:T(8,128)S(1)}, s32[128,128]{1,0:T(8,128)S(1)}, s32[]{:T(128)}, /*index=5*/s32[]{:T(128)}, s32[]{:T(128)}, s32[]{:T(128)}) while((s32[]{:T(128)}, s32[512,128]{1,0:T(8,128)S(1)}, s32[512,128]{1,0:T(8,128)S(1)}, s32[128,128]{1,0:T(8,128)S(1)}, s32[]{:T(128)}, ...), condition=%wide.region_5.6_spmd, body=%wide.region_3.5_spmd.sunk | while | flops 1048582 | bytes 1110155 | solution.py:30
  143.1 28.1 %all-gather.19.cloned.1.call-done = s32[2048,128]{1,0:T(8,128)} async-done(((s32[512,128]{1,0:T(8,128)}), s32[2048,128]{1,0:T(8,128)}) %all-gather.19.cloned.1.call-update) | async-done | bytes 1048592 | tf_op jit(solution)/shard_map/all_gather | solution.py:11
  172.5 123.8 %while.158 = (s32[]{:T(128)}, s32[512,1024]{1,0:T(8,128)S(1)}, s32[512,128]{1,0:T(8,128)S(1)}, s32[128,1024]{1,0:T(8,128)S(1)}, s32[]{:T(128)}, /*index=5*/s32[]{:T(128)}, s32[]{:T(128)}, s32[]{:T(128)}) while((s32[]{:T(128)}, s32[512,1024]{1,0:T(8,128)S(1)}, s32[512,128]{1,0:T(8,128)S(1)}, s32[128,1024]{1,0:T(8,128)S(1)}, s32[]{:T(128)}, ...), condition=%wide.region_9.10_spmd, body=%wide.region_7.9_spmd.sunk | while | flops 8388614 | bytes 8536203 | solution.py:30
  180.4 6.9 add_reduce_fusion.17
  188.1 6.9 add_reduce_fusion.17
  195.9 6.9 add_reduce_fusion.17
  203.6 6.9 add_reduce_fusion.17
  211.4 6.9 add_reduce_fusion.17
  219.1 6.9 add_reduce_fusion.17
  226.8 6.9 add_reduce_fusion.17
  257.8 6.9 add_reduce_fusion.17
  265.5 6.9 add_reduce_fusion.17
  273.2 6.9 add_reduce_fusion.17
  281.0 6.9 add_reduce_fusion.17
  288.7 6.9 add_reduce_fusion.17
  297.3 36.0 %all-gather.21.cloned.1.call-done = s32[1024,1024]{1,0:T(8,128)} async-done(((s32[128,1024]{1,0:T(8,128)}), s32[1024,1024]{1,0:T(8,128)}) %all-gather.21.cloned.1.call-update) | async-done | bytes 4194320 | tf_op jit(solution)/shard_map/all_gather | solution.py:11
  335.9 40.4 %while.159 = (s32[]{:T(128)}, s32[128,128]{1,0:T(8,128)S(1)}, s32[]{:T(128)}) while((s32[]{:T(128)}, s32[128,128]{1,0:T(8,128)S(1)}, s32[]{:T(128)}) %tuple.290), condition=%wide.region_12.13_spmd, body=%wide.region_11.12_spmd.sunk | while | flops 32770 | bytes 134197 | solution.py:41
  376.3 50.6 %while.160 = (s32[]{:T(128)}, s32[512,128]{1,0:T(8,128)S(1)}, s32[512,128]{1,0:T(8,128)S(1)}, s32[128,128]{1,0:T(8,128)S(1)}, s32[]{:T(128)}, /*index=5*/s32[]{:T(128)}, s32[]{:T(128)}, s32[]{:T(128)}) while((s32[]{:T(128)}, s32[512,128]{1,0:T(8,128)S(1)}, s32[512,128]{1,0:T(8,128)S(1)}, s32[128,128]{1,0:T(8,128)S(1)}, s32[]{:T(128)}, ...), condition=%wide.region_15.16_spmd, body=%wide.region_13.15_spmd.sunk | while | flops 1048582 | bytes 1110155 | solution.py:30
  427.7 28.1 %all-gather.23.cloned.1.call-done = s32[2048,128]{1,0:T(8,128)} async-done(((s32[512,128]{1,0:T(8,128)}), s32[2048,128]{1,0:T(8,128)}) %all-gather.23.cloned.1.call-update) | async-done | bytes 1048592 | tf_op jit(solution)/shard_map/all_gather | solution.py:11
  457.1 123.8 %while.161 = (s32[]{:T(128)}, s32[512,1024]{1,0:T(8,128)S(1)}, s32[512,128]{1,0:T(8,128)S(1)}, s32[128,1024]{1,0:T(8,128)S(1)}, s32[]{:T(128)}, /*index=5*/s32[]{:T(128)}, s32[]{:T(128)}, s32[]{:T(128)}) while((s32[]{:T(128)}, s32[512,1024]{1,0:T(8,128)S(1)}, s32[512,128]{1,0:T(8,128)S(1)}, s32[128,1024]{1,0:T(8,128)S(1)}, s32[]{:T(128)}, ...), condition=%wide.region_19.20_spmd, body=%wide.region_17.19_spmd.sunk | while | flops 8388614 | bytes 8536203 | solution.py:30
  582.1 35.8 %all-gather.25.cloned.1.call-done = s32[1024,1024]{1,0:T(8,128)} async-done(((s32[128,1024]{1,0:T(8,128)}), s32[1024,1024]{1,0:T(8,128)}) %all-gather.25.cloned.1.call-update) | async-done | bytes 4194320 | tf_op jit(solution)/shard_map/all_gather | solution.py:11
  620.5 40.4 %while.162 = (s32[]{:T(128)}, s32[128,128]{1,0:T(8,128)S(1)}, s32[]{:T(128)}) while((s32[]{:T(128)}, s32[128,128]{1,0:T(8,128)S(1)}, s32[]{:T(128)}) %tuple.299), condition=%wide.region_22.23_spmd, body=%wide.region_21.22_spmd.sunk | while | flops 32770 | bytes 134197 | solution.py:41
  660.9 50.6 %while.163 = (s32[]{:T(128)}, s32[512,128]{1,0:T(8,128)S(1)}, s32[512,128]{1,0:T(8,128)S(1)}, s32[128,128]{1,0:T(8,128)S(1)}, s32[]{:T(128)}, /*index=5*/s32[]{:T(128)}, s32[]{:T(128)}, s32[]{:T(128)}) while((s32[]{:T(128)}, s32[512,128]{1,0:T(8,128)S(1)}, s32[512,128]{1,0:T(8,128)S(1)}, s32[128,128]{1,0:T(8,128)S(1)}, s32[]{:T(128)}, ...), condition=%wide.region_25.26_spmd, body=%wide.region_23.25_spmd.sunk | while | flops 1048582 | bytes 1110155 | solution.py:30
  712.3 28.1 %all-gather.27.cloned.1.call-done = s32[2048,128]{1,0:T(8,128)} async-done(((s32[512,128]{1,0:T(8,128)}), s32[2048,128]{1,0:T(8,128)}) %all-gather.27.cloned.1.call-update) | async-done | bytes 1048592 | tf_op jit(solution)/shard_map/all_gather | solution.py:11
  741.7 123.8 %while.164 = (s32[]{:T(128)}, s32[512,1024]{1,0:T(8,128)S(1)}, s32[512,128]{1,0:T(8,128)S(1)}, s32[128,1024]{1,0:T(8,128)S(1)}, s32[]{:T(128)}, /*index=5*/s32[]{:T(128)}, s32[]{:T(128)}, s32[]{:T(128)}) while((s32[]{:T(128)}, s32[512,1024]{1,0:T(8,128)S(1)}, s32[512,128]{1,0:T(8,128)S(1)}, s32[128,1024]{1,0:T(8,128)S(1)}, s32[]{:T(128)}, ...), condition=%wide.region_29.30_spmd, body=%wide.region_27.29_spmd.sunk | while | flops 8388614 | bytes 8536203 | solution.py:30
  866.5 36.0 %all-gather.29.cloned.1.call-done = s32[1024,1024]{1,0:T(8,128)} async-done(((s32[128,1024]{1,0:T(8,128)}), s32[1024,1024]{1,0:T(8,128)}) %all-gather.29.cloned.1.call-update) | async-done | bytes 4194320 | tf_op jit(solution)/shard_map/all_gather | solution.py:11
  905.1 40.4 %while.165 = (s32[]{:T(128)}, s32[128,128]{1,0:T(8,128)S(1)}, s32[]{:T(128)}) while((s32[]{:T(128)}, s32[128,128]{1,0:T(8,128)S(1)}, s32[]{:T(128)}) %tuple.308), condition=%wide.region_32.33_spmd, body=%wide.region_31.32_spmd.sunk | while | flops 32770 | bytes 134197 | solution.py:41
  945.5 50.6 %while.166 = (s32[]{:T(128)}, s32[512,128]{1,0:T(8,128)S(1)}, s32[512,128]{1,0:T(8,128)S(1)}, s32[128,128]{1,0:T(8,128)S(1)}, s32[]{:T(128)}, /*index=5*/s32[]{:T(128)}, s32[]{:T(128)}, s32[]{:T(128)}) while((s32[]{:T(128)}, s32[512,128]{1,0:T(8,128)S(1)}, s32[512,128]{1,0:T(8,128)S(1)}, s32[128,128]{1,0:T(8,128)S(1)}, s32[]{:T(128)}, ...), condition=%wide.region_35.36_spmd, body=%wide.region_33.35_spmd.sunk | while | flops 1048582 | bytes 1110155 | solution.py:30
  996.8 28.1 %all-gather.31.cloned.1.call-done = s32[2048,128]{1,0:T(8,128)} async-done(((s32[512,128]{1,0:T(8,128)}), s32[2048,128]{1,0:T(8,128)}) %all-gather.31.cloned.1.call-update) | async-done | bytes 1048592 | tf_op jit(solution)/shard_map/all_gather | solution.py:11
  1026.3 123.8 %while.167 = (s32[]{:T(128)}, s32[512,1024]{1,0:T(8,128)S(1)}, s32[512,128]{1,0:T(8,128)S(1)}, s32[128,1024]{1,0:T(8,128)S(1)}, s32[]{:T(128)}, /*index=5*/s32[]{:T(128)}, s32[]{:T(128)}, s32[]{:T(128)}) while((s32[]{:T(128)}, s32[512,1024]{1,0:T(8,128)S(1)}, s32[512,128]{1,0:T(8,128)S(1)}, s32[128,1024]{1,0:T(8,128)S(1)}, s32[]{:T(128)}, ...), condition=%wide.region_39.40_spmd, body=%wide.region_37.39_spmd.sunk | while | flops 8388614 | bytes 8536203 | solution.py:30
  (2085 shorter events, 777.6 us)
Async XLA Ops:
  6.5 42.1 %all-gather.17.cloned.1.call-start = ((), (), s32[]{:S(2)}) async-start(), calls=%async_computation | async-start | bytes 4718592 | tf_op jit(solution)/shard_map/all_gather | solution.py:11
  9.2 162.0 %all-gather.19.cloned.1.call-start = ((), (), s32[]{:S(2)}) async-start(), calls=%async_computation.1 | async-start | bytes 1310720 | tf_op jit(solution)/shard_map/all_gather | solution.py:11
  143.1 190.2 %all-gather.21.cloned.1.call-start = ((), (), s32[]{:S(2)}) async-start(), calls=%async_computation.2 | async-start | bytes 4718592 | tf_op jit(solution)/shard_map/all_gather | solution.py:11
  297.2 158.6 %all-gather.23.cloned.1.call-start = ((), (), s32[]{:S(2)}) async-start(), calls=%async_computation.3 | async-start | bytes 1310720 | tf_op jit(solution)/shard_map/all_gather | solution.py:11
  427.7 190.2 %all-gather.25.cloned.1.call-start = ((), (), s32[]{:S(2)}) async-start(), calls=%async_computation.4 | async-start | bytes 4718592 | tf_op jit(solution)/shard_map/all_gather | solution.py:11
  581.8 158.6 %all-gather.27.cloned.1.call-start = ((), (), s32[]{:S(2)}) async-start(), calls=%async_computation.5 | async-start | bytes 1310720 | tf_op jit(solution)/shard_map/all_gather | solution.py:11
  712.2 190.2 %all-gather.29.cloned.1.call-start = ((), (), s32[]{:S(2)}) async-start(), calls=%async_computation.6 | async-start | bytes 4718592 | tf_op jit(solution)/shard_map/all_gather | solution.py:11
  866.4 158.6 %all-gather.31.cloned.1.call-start = ((), (), s32[]{:S(2)}) async-start(), calls=%async_computation.7 | async-start | bytes 1310720 | tf_op jit(solution)/shard_map/all_gather | solution.py:11
  1150.1 1.3 copy-start
Sparse Core Ops, SparseCore 0:
  9.3 39.2 all-gather.16
  143.2 27.9 all-gather.18
  297.3 35.9 all-gather.20
  427.8 27.9 all-gather.22
  581.9 35.9 all-gather.24
  712.4 27.9 all-gather.26
  866.5 35.9 all-gather.28
  997.0 27.9 all-gather.30
